TPU v7x, 128 devices: a whole 4x4x4 slice. The times are simulated.
128 devices in a mesh: rows: 8 (over z, core), model: 16 (over y, x).
Axes of the slice: x: 4, y: 4, z: 4, core: 2. Of those that a mesh axis runs over, the one named last changes fastest.
Arguments:
- train_query: bfloat16 [8192, 8192], P('rows', 'model'), may hold values from -0.0625 to 0.0625
- low_query: bfloat16 [8192, 16], P('rows'), may hold values from -0.0625 to 0.0625
- high_query: bfloat16 [16, 8192], P(None, 'model'), may hold values from -1.5 to 1.5
- train_key: bfloat16 [8192, 1024], P('rows', 'model'), may hold values from -0.0625 to 0.0625
- low_key: bfloat16 [8192, 16], P('rows'), may hold values from -0.0625 to 0.0625
- high_key: bfloat16 [16, 1024], P(None, 'model'), may hold values from -1.5 to 1.5
- train_value: bfloat16 [8192, 1024], P('rows', 'model'), may hold values from -0.0625 to 0.0625
- low_value: bfloat16 [8192, 16], P('rows'), may hold values from -0.0625 to 0.0625
- high_value: bfloat16 [16, 1024], P(None, 'model'), may hold values from -1.5 to 1.5
- train_mixed: bfloat16 [8192, 8192], P('model', 'rows'), may hold values from -0.0625 to 0.0625
- low_mixed: bfloat16 [8192, 16], P('model'), may hold values from -0.0625 to 0.0625
- high_mixed: bfloat16 [16, 8192], P(None, 'rows'), may hold values from -1.5 to 1.5
- norm_train: float32 [8192], P(('rows', 'model')), may hold values from 0.25 to 1.75
- norm_step: float32 [8192], P(('rows', 'model')), may hold values from -0.3 to 0.3
Outputs:
- serving_query: bfloat16 [8192, 8192], P('model')
- serving_key: bfloat16 [1024, 8192], P('model')
- serving_value: bfloat16 [1024, 8192], P('model')
- serving_mixed: bfloat16 [8192, 8192], P(None, 'model')
- serve_norm: bfloat16 [8192], replicated
All inputs are finite; a program needn't handle non-finite values.
Results may differ from a plain program's by a relative error of at most 0.001.
Values may be sent and summed in bfloat16 or wider, within the bound.
A program may use at most 128 MiB of HBM per device.

v0:
```python
import jax
import jax.numpy as jnp
from jax import lax
from jax.sharding import Mesh
from jax.sharding import PartitionSpec as P

ROWS = ("rows_0", "rows_1")
ROWS_MODEL = ("rows_0", "rows_1", "model_0", "model_1")
MODEL = ("model_0", "model_1")
mix_rate = 0.5


def turned_gather(arrays, axis, dims):
    turned = [jnp.moveaxis(a, dim, 0) for a, dim in zip(arrays, dims)]
    widths = [t[0].size for t in turned]
    both = jnp.concatenate([t.reshape(-1, w) for t, w in zip(turned, widths)], axis=1)
    out = lax.all_gather(both, axis, axis=0, tiled=True)
    parts = jnp.split(out, [sum(widths[:k]) for k in range(1, len(widths))], axis=1)
    return tuple(
        (
            jnp.moveaxis(b.reshape(-1, *t.shape[1:]), 0, dim)
            for b, t, dim in zip(parts, turned, dims)
        )
    )


def in_order(parts, dim):
    parts = jnp.moveaxis(parts, 0, dim)
    shape = parts.shape
    return parts.reshape(*shape[:dim], shape[dim] * shape[dim + 1], *shape[dim + 2 :])


def stacked_from(array, axes, order):
    parts = array
    for k in order:
        parts = lax.all_gather(parts, axes[k])
    done = order[::-1]
    back = [done.index(k) for k in range(len(axes))]
    parts = parts.transpose(*back, *range(len(axes), parts.ndim))
    return parts.reshape(-1, *array.shape)


def whole_of(array, axes, order, dim):
    return in_order(stacked_from(array, axes, order), dim)


def body(
    train_query,
    low_query,
    high_query,
    train_key,
    low_key,
    high_key,
    train_value,
    low_value,
    high_value,
    train_mixed,
    low_mixed,
    high_mixed,
    norm_train,
    norm_step,
):
    whole_query = train_query.astype(jnp.float32) + mix_rate * jnp.dot(
        low_query, high_query, preferred_element_type=jnp.float32
    )
    whole_key = train_key.astype(jnp.float32) + mix_rate * jnp.dot(
        low_key, high_key, preferred_element_type=jnp.float32
    )
    whole_value = train_value.astype(jnp.float32) + mix_rate * jnp.dot(
        low_value, high_value, preferred_element_type=jnp.float32
    )
    whole_mixed = train_mixed.astype(jnp.float32) + mix_rate * jnp.dot(
        low_mixed, high_mixed, preferred_element_type=jnp.float32
    )
    narrow_query, narrow_key, narrow_value, narrow_mixed = (
        whole_query.astype(jnp.bfloat16),
        whole_key.astype(jnp.bfloat16),
        whole_value.astype(jnp.bfloat16),
        whole_mixed.astype(jnp.bfloat16),
    )
    serving_query, serving_key, serving_value, serving_mixed = turned_gather(
        (narrow_query, narrow_key, narrow_value, narrow_mixed), ROWS, (0, 0, 0, 1)
    )
    serving_query, serving_key, serving_value, serving_mixed = (
        serving_query.T,
        serving_key.T,
        serving_value.T,
        serving_mixed.T,
    )
    serve_norm = whole_of(
        (norm_train + norm_step).astype(jnp.bfloat16), ROWS_MODEL, (0, 2, 3, 1), 0
    )
    return (serving_query, serving_key, serving_value, serving_mixed, serve_norm)


def solution(mesh):
    finer = Mesh(mesh.devices.reshape(4, 2, 4, 4), ("rows_0", "rows_1", "model_0", "model_1"))
    return jax.shard_map(
        body,
        mesh=finer,
        in_specs=(
            P(ROWS, MODEL),
            P(ROWS, None),
            P(None, MODEL),
            P(ROWS, MODEL),
            P(ROWS, None),
            P(None, MODEL),
            P(ROWS, MODEL),
            P(ROWS, None),
            P(None, MODEL),
            P(MODEL, ROWS),
            P(MODEL, None),
            P(None, ROWS),
            P(ROWS_MODEL),
            P(ROWS_MODEL),
        ),
        out_specs=(P(MODEL, None), P(MODEL, None), P(MODEL, None), P(None, MODEL), P()),
        check_vma=False,
    )
```

profile of v0, /device:TPU:1, one launch (start us, length us, event | category | flops | bytes accessed | tf_op | source)
XLA Modules:
  0.0 144.0 jit_solution(17631566383366275951)
XLA Ops:
  7.2 0.0 copy-start
  7.2 0.0 copy-start.1
  7.2 0.0 copy-start.5
  7.2 0.0 copy-start.8
  7.2 0.0 copy-start.2
  7.2 0.0 copy-start.6
  7.2 0.0 copy-start.9
  7.2 0.0 copy-start.3
  7.3 0.0 all-gather.7.cloned.1.call-start
  7.3 1.6 %copy.35 = bf16[1024,512]{0,1:T(8,128)(2,1)S(1)} copy(bf16[1024,512]{1,0:T(8,128)(2,1)} %param.14) | data formatting | bytes 2097152 | tf_op args[0]
  8.9 1.2 fusion
  10.1 0.2 fusion.4
  10.4 0.0 copy-done.6
  10.4 0.0 copy-done.9
  10.4 0.0 copy-done.3
  10.4 0.2 fusion.3
  10.6 0.5 add_convert_fusion.1
  11.1 1.6 %pad_maximum_fusion = bf16[1024,1152]{0,1:T(8,128)(2,1)} fusion(bf16[1024,512]{0,1:T(8,128)(2,1)S(1)} %fusion, bf16[1024,64]{0,1:T(8,128)(2,1)S(1)} %fusion.4, bf16[1024,64]{0,1:T(8,128)(2,1)S(1)} %fusion.3, bf16[1024,512]{0,1:T(8,128)(2,1)S(1)} %add_convert_fusion.1), kind=kLoop, calls=%fused_computation.1 | loop fusion | flops 9437184 | bytes 4718592 | tf_op jit(solution)/shard_map/concatenate | solution.py:16
  12.7 0.0 all-gather.7.cloned.1.call-update
  12.8 0.6 copy-done.12
  13.4 0.6 dynamic-slice
  14.7 0.2 dynamic-update-slice
  14.9 10.5 %all-reduce = bf16[256]{0:T(256)(128)(2,1)S(1)} all-reduce(bf16[256]{0:T(256)(128)(2,1)S(1)} %dynamic-update-slice), channel_id=2, replica_groups=mesh['rows_0'=4,'rows_1'=2,'model_0'=4,'model_1'=4] {'rows_0'}, use_global_device_ids=true, to_apply=%add | all-reduce | flops 256 | bytes 1024
  25.5 0.1 reshape.17
  25.5 8.4 %all-gather.4 = bf16[4,4,64]{2,1,0:T(4,128)(2,1)S(1)} all-gather(bf16[1,4,64]{2,1,0:T(4,128)(2,1)S(1)} %reshape.17), channel_id=3, replica_groups=mesh['rows_0'=4,'rows_1'=2,'model_0'=4,'model_1'=4] {'model_0'}, dimensions={0}, use_global_device_ids=true | all-gather | bytes 2560 | tf_op jit(solution)/shard_map/all_gather | solution.py:36
  33.9 10.4 %all-gather.2 = bf16[16,4,64]{2,1,0:T(4,128)(2,1)S(1)} all-gather(bf16[4,4,64]{2,1,0:T(4,128)(2,1)S(1)} %all-gather.4), channel_id=4, replica_groups=mesh['rows_0'=4,'rows_1'=2,'model_0'=4,'model_1'=4] {'model_1'}, dimensions={0}, use_global_device_ids=true | all-gather | bytes 10240 | tf_op jit(solution)/shard_map/all_gather | solution.py:36
  44.3 7.7 %all-gather.3 = bf16[8,4,4,64]{3,1,0,2:T(4,128)(2,1)S(1)} all-gather(bf16[4,4,4,64]{3,1,0,2:T(4,128)(2,1)S(1)} %bitcast.22), channel_id=5, replica_groups=mesh['rows_0'=4,'rows_1'=2,'model_0'=4,'model_1'=4] {'rows_1'}, dimensions={0}, use_global_device_ids=true | all-gather | bytes 24576 | tf_op jit(solution)/shard_map/all_gather | solution.py:36
  52.1 0.7 reshape_reshape.3
  52.8 57.7 %all-gather.7.cloned.1.call-done = bf16[8192,1152]{0,1:T(8,128)(2,1)} async-done(((bf16[1024,1152]{0,1:T(8,128)(2,1)}), bf16[8192,1152]{0,1:T(8,128)(2,1)}) %all-gather.7.cloned.1.call-update) | async-done | bytes 18874384 | tf_op jit(solution)/shard_map/all_gather | solution.py:17
  110.5 11.7 %fusion.5 = (bf16[8192,512]{0,1:T(8,128)(2,1)}, bf16[512,8192]{1,0:T(8,128)(2,1)}) fusion(bf16[8192,1152]{0,1:T(8,128)(2,1)} %all-gather.7.cloned.1.call-done), kind=kLoop, calls=%fused_computation.14 | loop fusion | bytes 33554432 | tf_op jit(solution)/shard_map/split | solution.py:18
  122.1 11.9 %copy.39 = bf16[8192,512]{1,0:T(8,128)(2,1)} copy(bf16[8192,512]{0,1:T(8,128)(2,1)} %get-tuple-element.35) | data formatting | bytes 16777216
  134.1 3.0 %slice_bitcast_fusion.1 = (bf16[64,8192]{1,0:T(8,128)(2,1)}, bf16[64,8192]{1,0:T(8,128)(2,1)}) fusion(bf16[8192,1152]{0,1:T(8,128)(2,1)} %all-gather.7.cloned.1.call-done), kind=kLoop, calls=%fused_computation.11 | loop fusion | bytes 4194304 | tf_op jit(solution)/shard_map/transpose | solution.py:87
  (19 shorter events, 0.1 us)
Async XLA Ops:
  7.2 1.7 %copy-start = (bf16[16,1024]{1,0:T(8,128)(2,1)S(1)}, bf16[16,1024]{1,0:T(8,128)(2,1)}, u32[]{:S(2)}) copy-start(bf16[16,1024]{1,0:T(8,128)(2,1)} %param.25) | copy-start | bytes 98308
  7.2 1.7 %copy-start.1 = (bf16[512,1024]{1,0:T(8,128)(2,1)S(1)}, bf16[512,1024]{1,0:T(8,128)(2,1)}, u32[]{:S(2)}) copy-start(bf16[512,1024]{1,0:T(8,128)(2,1)} %param.23) | copy-start | bytes 3145732
  7.2 2.9 %copy-start.5 = (bf16[1024,16]{0,1:T(8,128)(2,1)S(1)}, bf16[1024,16]{0,1:T(8,128)(2,1)}, u32[]{:S(2)}) copy-start(bf16[1024,16]{0,1:T(8,128)(2,1)} %param.21) | copy-start | bytes 98308
  7.2 2.9 %copy-start.8 = (bf16[16,64]{1,0:T(8,128)(2,1)S(1)}, bf16[16,64]{1,0:T(8,128)(2,1)}, u32[]{:S(2)}) copy-start(bf16[16,64]{1,0:T(8,128)(2,1)} %param.22) | copy-start | bytes 6148
  7.2 2.9 %copy-start.2 = (bf16[1024,64]{0,1:T(8,128)(2,1)S(1)}, bf16[1024,64]{0,1:T(8,128)(2,1)}, u32[]{:S(2)}) copy-start(bf16[1024,64]{0,1:T(8,128)(2,1)} %param.20) | copy-start | bytes 393220
  7.2 3.1 %copy-start.6 = (bf16[1024,16]{0,1:T(8,128)(2,1)S(1)}, bf16[1024,16]{0,1:T(8,128)(2,1)}, u32[]{:S(2)}) copy-start(bf16[1024,16]{0,1:T(8,128)(2,1)} %param.18) | copy-start | bytes 98308
  7.2 3.1 %copy-start.9 = (bf16[16,64]{1,0:T(8,128)(2,1)S(1)}, bf16[16,64]{1,0:T(8,128)(2,1)}, u32[]{:S(2)}) copy-start(bf16[16,64]{1,0:T(8,128)(2,1)} %param.19) | copy-start | bytes 6148
  7.2 3.1 %copy-start.3 = (bf16[1024,64]{0,1:T(8,128)(2,1)S(1)}, bf16[1024,64]{0,1:T(8,128)(2,1)}, u32[]{:S(2)}) copy-start(bf16[1024,64]{0,1:T(8,128)(2,1)} %param.17) | copy-start | bytes 393220
  7.3 3.4 %copy-start.4 = (bf16[1024,16]{0,1:T(8,128)(2,1)S(1)}, bf16[1024,16]{0,1:T(8,128)(2,1)}, u32[]{:S(2)}) copy-start(bf16[1024,16]{0,1:T(8,128)(2,1)} %param.15) | copy-start | bytes 98308
  7.3 3.4 %copy-start.7 = (bf16[16,512]{1,0:T(8,128)(2,1)S(1)}, bf16[16,512]{1,0:T(8,128)(2,1)}, u32[]{:S(2)}) copy-start(bf16[16,512]{1,0:T(8,128)(2,1)} %param.16) | copy-start | bytes 49156
  7.3 103.2 %all-gather.7.cloned.1.call-start = ((), (), s32[]{:S(2)}) async-start(), calls=%async_computation | async-start | bytes 21233664 | tf_op jit(solution)/shard_map/all_gather | solution.py:17
  12.7 0.7 copy-start.12
  12.7 1.9 %copy-start.10 = (f32[64]{0:T(128)S(1)}, f32[64]{0:T(128)}, u32[]{:S(2)}) copy-start(f32[64]{0:T(128)} %param.26) | copy-start | bytes 772
  12.7 1.9 %copy-start.11 = (f32[64]{0:T(128)S(1)}, f32[64]{0:T(128)}, u32[]{:S(2)}) copy-start(f32[64]{0:T(128)} %param.27) | copy-start | bytes 772
Sparse Core Ops, SparseCore 0:
  12.9 97.5 all-gather.6
where the time goes:
time: 145 us; the launch traced here: 144 us
  waiting for transfers between devices  57.7 us (40%)
  blocking collectives  37 us (26%)
  local copies, waits for them, and re-layouts  30.5 us (21%)
  between operations  14.9 us (10%)
  matrix products  2.1 us (1%)
  other arithmetic  1.62 us (1%)
    all_gather x1, waiting for transfers between devices, turned_gather(): out = lax.all_gather(both, axis, axis=0, tiled=True)  57.7 us
    all_gather x3, blocking collectives, stacked_from(): parts = lax.all_gather(parts, axes[k])  26.5 us
    unnamed x32, local copies, waits for them, and re-layouts  15.1 us
    split x1, local copies, waits for them, and re-layouts, turned_gather(): jnp.split(out, [sum(widths[:k]) for k in range(1, len(widths))], axis=1)  11.7 us
    unnamed x1, blocking collectives  10.5 us
    transpose x1, local copies, waits for them, and re-layouts, body(): serving_query, serving_key, serving_value, serving_mixed = (serving_query...  3.04 us
  transfers between devices with their start and end apart: 1, of which 1 were waited for; matrix products, arithmetic and copies ran while one was open for 1% of the time, Pallas kernels for 0%

commit v1 on v0

--- a/solution.py
+++ b/solution.py
@@ -14,7 +14,9 @@
     turned = [jnp.moveaxis(a, dim, 0) for a, dim in zip(arrays, dims)]
     widths = [t[0].size for t in turned]
     both = jnp.concatenate([t.reshape(-1, w) for t, w in zip(turned, widths)], axis=1)
-    out = lax.all_gather(both, axis, axis=0, tiled=True)
+    out = jnp.concatenate(
+        lax.all_to_all(jnp.stack([both] * lax.axis_size(axis)), axis, 0, 0), axis=0
+    )
     parts = jnp.split(out, [sum(widths[:k]) for k in range(1, len(widths))], axis=1)
     return tuple(
         (

time: 145 us -> 289 us (1.99)
  blocking collectives: 37 us -> 232 us
  waiting for transfers between devices: 57.7 us -> 0.01 us
  local copies, waits for them, and re-layouts: 30.5 us -> 45.7 us
  between operations: 14.9 us -> 1.5 us
  starting transfers between devices: 0.04 us -> 7.31 us
    unnamed x1, blocking collectives: 10.5 us -> 206 us
    all_gather x1 -> x0, waiting for transfers between devices: 57.7 us -> none  [turned_gather(): out = lax.all_gather(both, axis, axis=0, tiled=True)]
    another operation x0 -> x1, local copies, waits for them, and re-layouts: none -> 7.76 us  [turned_gather(): jnp.stack([both] * lax.axis_size(axis))]
    all_to_all x0 -> x1, starting transfers between devices: none -> 7.31 us  [turned_gather(): lax.all_to_all(jnp.stack([both] * lax.axis_size(axis)), axis, 0, 0)]
    unnamed x32, local copies, waits for them, and re-layouts: 15.1 us -> 18.8 us
  transfers between devices with their start and end apart: 1 -> 1, of which waited for: 1 -> 0; matrix products, arithmetic and copies ran while one was open for 1% -> 1% of each run, Pallas kernels for 0% -> 0%
where the time goes in v1:
time: 289 us
  blocking collectives  232 us (80%)
  local copies, waits for them, and re-layouts  45.7 us (16%)
  starting transfers between devices  7.31 us (3%)
    unnamed x1, blocking collectives  206 us
    all_gather x3, blocking collectives, stacked_from(): parts = lax.all_gather(parts, axes[k])  25.7 us
    unnamed x32, local copies, waits for them, and re-layouts  18.8 us
    split x1, local copies, waits for them, and re-layouts, turned_gather(): jnp.split(out, [sum(widths[:k]) for k in range(1, len(widths))], axis=1)  11.5 us
    another operation x1, local copies, waits for them, and re-layouts, turned_gather(): jnp.stack([both] * lax.axis_size(axis))  7.76 us
    all_to_all x1, starting transfers between devices, turned_gather(): lax.all_to_all(jnp.stack([both] * lax.axis_size(axis)), axis, 0, 0)  7.31 us
  transfers between devices with their start and end apart: 1, of which 0 were waited for; matrix products, arithmetic and copies ran while one was open for 1% of the time, Pallas kernels for 0%

profile of v1, /device:TPU:1, one launch (start us, length us, event | category | flops | bytes accessed | tf_op | source)
XLA Modules:
  0.0 288.8 jit_solution(1488727271037197386)
XLA Ops:
  0.6 0.0 copy-start
  0.7 0.0 copy-start.8
  0.7 0.0 copy-start.5
  0.7 0.0 copy-start.3
  0.7 0.0 copy-start.6
  0.7 0.0 copy-start.4
  0.7 0.0 copy-start.7
  0.7 0.0 copy-start.2
  0.7 1.6 copy.50
  2.4 1.2 fusion.3
  3.6 0.2 fusion.4
  3.8 0.5 add_convert_fusion.1
  4.3 0.5 fusion
  4.8 0.2 pad_maximum_fusion
  5.0 2.4 copy.51
  7.4 7.8 %stack.2 = bf16[8,1024,1152]{2,1,0:T(8,128)(2,1)} broadcast(bf16[1024,1152]{1,0:T(8,128)(2,1)} %copy.51), dimensions={1,2} | broadcast | bytes 21233664 | tf_op jit(solution)/shard_map/stack | solution.py:18
  15.2 7.3 %all-to-all-start = ((bf16[8,1024,1152]{2,1,0:T(8,128)(2,1)}), bf16[8,1024,1152]{2,1,0:T(8,128)(2,1)}, u32[]{:S(2)}, u32[]{:S(2)}) async-start(bf16[8,1024,1152]{2,1,0:T(8,128)(2,1)} %stack.2), calls=%async_computation | async-start | bytes 37748736 | tf_op jit(solution)/shard_map/all_to_all | solution.py:18
  22.5 0.0 copy-done.11
  22.5 0.6 dynamic-slice
  23.8 0.2 dynamic-update-slice
  24.0 206.0 %all-reduce = bf16[256]{0:T(256)(128)(2,1)S(1)} all-reduce(bf16[256]{0:T(256)(128)(2,1)S(1)} %dynamic-update-slice), channel_id=2, replica_groups=mesh['rows_0'=4,'rows_1'=2,'model_0'=4,'model_1'=4] {'rows_0'}, use_global_device_ids=true, to_apply=%add | all-reduce | flops 256 | bytes 1024
  230.1 0.1 reshape.23
  230.2 7.9 %all-gather.4 = bf16[4,4,64]{2,1,0:T(4,128)(2,1)S(1)} all-gather(bf16[1,4,64]{2,1,0:T(4,128)(2,1)S(1)} %reshape.23), channel_id=3, replica_groups=mesh['rows_0'=4,'rows_1'=2,'model_0'=4,'model_1'=4] {'model_0'}, dimensions={0}, use_global_device_ids=true | all-gather | bytes 2560 | tf_op jit(solution)/shard_map/all_gather | solution.py:38
  238.1 9.5 %all-gather.2 = bf16[16,4,64]{2,1,0:T(4,128)(2,1)S(1)} all-gather(bf16[4,4,64]{2,1,0:T(4,128)(2,1)S(1)} %all-gather.4), channel_id=4, replica_groups=mesh['rows_0'=4,'rows_1'=2,'model_0'=4,'model_1'=4] {'model_1'}, dimensions={0}, use_global_device_ids=true | all-gather | bytes 10240 | tf_op jit(solution)/shard_map/all_gather | solution.py:38
  247.6 8.3 %all-gather.3 = bf16[8,4,4,64]{3,1,0,2:T(4,128)(2,1)S(1)} all-gather(bf16[4,4,4,64]{3,1,0,2:T(4,128)(2,1)S(1)} %bitcast.23), channel_id=5, replica_groups=mesh['rows_0'=4,'rows_1'=2,'model_0'=4,'model_1'=4] {'rows_1'}, dimensions={0}, use_global_device_ids=true | all-gather | bytes 24576 | tf_op jit(solution)/shard_map/all_gather | solution.py:38
  255.9 0.7 reshape_reshape.3
  256.6 0.0 all-to-all-done
  256.6 4.4 %slice_bitcast_fusion.1 = (bf16[64,8192]{0,1:T(8,128)(2,1)}, bf16[64,8192]{0,1:T(8,128)(2,1)S(1)}) fusion(bf16[8192,1152]{1,0:T(8,128)(2,1)} %bitcast.1), kind=kLoop, calls=%fused_computation.2 | loop fusion | bytes 4194304 | tf_op jit(solution)/shard_map/transpose | solution.py:89
  261.1 11.5 %fusion.5 = (bf16[8192,512]{1,0:T(8,128)(2,1)}, bf16[512,8192]{0,1:T(8,128)(2,1)}) fusion(bf16[8192,1152]{1,0:T(8,128)(2,1)} %bitcast.1), kind=kLoop, calls=%fused_computation.14 | loop fusion | bytes 33554432 | tf_op jit(solution)/shard_map/split | solution.py:20
  272.6 2.7 copy.57
  275.3 1.6 copy.56
  276.9 11.9 %copy.55 = bf16[512,8192]{1,0:T(8,128)(2,1)} copy(bf16[512,8192]{0,1:T(8,128)(2,1)} %get-tuple-element.36) | data formatting | bytes 16777216
  (20 shorter events, 0.1 us)
Async XLA Ops:
  0.6 3.2 %copy-start = (bf16[1024,16]{0,1:T(8,128)(2,1)S(1)}, bf16[1024,16]{0,1:T(8,128)(2,1)}, u32[]{:S(2)}) copy-start(bf16[1024,16]{0,1:T(8,128)(2,1)} %param.15) | copy-start | bytes 98308
  0.7 2.9 %copy-start.8 = (bf16[16,64]{1,0:T(8,128)(2,1)S(1)}, bf16[16,64]{1,0:T(8,128)(2,1)}, u32[]{:S(2)}) copy-start(bf16[16,64]{1,0:T(8,128)(2,1)} %param.22) | copy-start | bytes 6148
  0.7 2.9 %copy-start.5 = (bf16[1024,16]{0,1:T(8,128)(2,1)S(1)}, bf16[1024,16]{0,1:T(8,128)(2,1)}, u32[]{:S(2)}) copy-start(bf16[1024,16]{0,1:T(8,128)(2,1)} %param.21) | copy-start | bytes 98308
  0.7 2.9 %copy-start.3 = (bf16[1024,64]{0,1:T(8,128)(2,1)S(1)}, bf16[1024,64]{0,1:T(8,128)(2,1)}, u32[]{:S(2)}) copy-start(bf16[1024,64]{0,1:T(8,128)(2,1)} %param.20) | copy-start | bytes 393220
  0.7 3.1 %copy-start.6 = (bf16[16,512]{1,0:T(8,128)(2,1)S(1)}, bf16[16,512]{1,0:T(8,128)(2,1)}, u32[]{:S(2)}) copy-start(bf16[16,512]{1,0:T(8,128)(2,1)} %param.16) | copy-start | bytes 49156
  0.7 3.6 %copy-start.4 = (bf16[16,1024]{1,0:T(8,128)(2,1)S(1)}, bf16[16,1024]{1,0:T(8,128)(2,1)}, u32[]{:S(2)}) copy-start(bf16[16,1024]{1,0:T(8,128)(2,1)} %param.25) | copy-start | bytes 98308
  0.7 3.6 %copy-start.7 = (bf16[512,16]{0,1:T(8,128)(2,1)S(1)}, bf16[512,16]{0,1:T(8,128)(2,1)}, u32[]{:S(2)}) copy-start(bf16[512,16]{0,1:T(8,128)(2,1)} %param.24) | copy-start | bytes 49156
  0.7 3.6 %copy-start.2 = (bf16[512,1024]{1,0:T(8,128)(2,1)S(1)}, bf16[512,1024]{1,0:T(8,128)(2,1)}, u32[]{:S(2)}) copy-start(bf16[512,1024]{1,0:T(8,128)(2,1)} %param.23) | copy-start | bytes 3145732
  15.2 7.3 %copy-start.11 = (u32[128]{0:T(128)S(1)}, u32[128]{0:T(128)}, u32[]{:S(2)}) copy-start(u32[128]{0:T(128)} %constant.8) | copy-start | bytes 1540
  15.2 8.6 %copy-start.9 = (f32[64]{0:T(128)S(1)}, f32[64]{0:T(128)}, u32[]{:S(2)}) copy-start(f32[64]{0:T(128)} %param.26) | copy-start | bytes 772
  15.2 8.6 %copy-start.10 = (f32[64]{0:T(128)S(1)}, f32[64]{0:T(128)}, u32[]{:S(2)}) copy-start(f32[64]{0:T(128)} %param.27) | copy-start | bytes 772
  15.2 241.4 %all-to-all-start = ((bf16[8,1024,1152]{2,1,0:T(8,128)(2,1)}), bf16[8,1024,1152]{2,1,0:T(8,128)(2,1)}, u32[]{:S(2)}, u32[]{:S(2)}) async-start(bf16[8,1024,1152]{2,1,0:T(8,128)(2,1)} %stack.2), calls=%async_computation | async-start | bytes 37748736 | tf_op jit(solution)/shard_map/all_to_all | solution.py:18
  276.9 11.9 %copy-start.1 = (bf16[1024,16]{0,1:T(8,128)(2,1)S(1)}, bf16[1024,16]{0,1:T(8,128)(2,1)}, u32[]{:S(2)}) copy-start(bf16[1024,16]{0,1:T(8,128)(2,1)} %param.15) | copy-start | bytes 98308
